TPU v7x, 32 devices: a whole 2x2x4 slice. The times are simulated.
32 devices in a mesh: parts: 2 (over y), rows: 4 (over z), cols: 2 (over x), rank: 2 (over core).
Axes of the slice: x: 2, y: 2, z: 4, core: 2. Of those that a mesh axis runs over, the one named last changes fastest.
Arguments:
- probes: bfloat16 [32768, 128], P(('parts', 'rows', 'cols')), parts along dimension 0, may hold values from -6 to 6
- basis_one: bfloat16 [32768, 256], P(('parts', 'rows', 'cols'), 'rank'), parts along dimension 0, may hold values from -0.375 to 0.375
- basis_two: bfloat16 [32768, 256], P(('parts', 'rows', 'cols'), 'rank'), parts along dimension 0, may hold values from -0.375 to 0.375
- basis_three: bfloat16 [32768, 256], P(('parts', 'rows', 'cols'), 'rank'), parts along dimension 0, may hold values from -0.375 to 0.375
- coeff_one: bfloat16 [32768, 256], P(('parts', 'rows', 'cols'), 'rank'), parts along dimension 0, may hold values from -0.0625 to 0.0625
- coeff_two: bfloat16 [32768, 256], P(('parts', 'rows', 'cols'), 'rank'), parts along dimension 0, may hold values from -0.09375 to 0.09375
- coeff_three: bfloat16 [32768, 256], P(('parts', 'rows', 'cols'), 'rank'), parts along dimension 0, may hold values from -0.125 to 0.125
- leaves: bfloat16 [128, 256, 256], P(('parts', 'rows', 'cols', 'rank')), parts along dimension 0, may hold values from -0.375 to 0.375
Outputs:
- covariance_power: bfloat16 [32768, 128], P(('parts', 'rows', 'cols', 'rank')), parts along dimension 0
There are 2 independent parts, one for each index of `parts`. A program takes and returns all parts, laid end to end along the dimension named above; each array names one. Nothing has to cross between parts.
All inputs are finite; a program needn't handle non-finite values.
Results may differ from a plain program's by a relative error of at most 0.017.
Values may be sent and summed in bfloat16 or wider, within the bound.
A program may use at most 64 MiB of HBM per device.

v0:
```python
import jax
import jax.numpy as jnp
from jax import lax
from jax.sharding import PartitionSpec as P

C = 128
LEAF = 256
PASSES = 2


def as_sent(x):
    return jax.tree.map(lambda a: a.astype(jnp.bfloat16) if a.dtype == jnp.float32 else a, x)


def partner(value, axis, stride):
    mask = 2**stride
    pairs = [(source, source ^ mask) for source in range(lax.axis_size(axis))]
    return lax.ppermute(value, axis, pairs)


def combine_levels(projections):
    total_bits = lax.axis_size(("rows", "cols")).bit_length() - 1
    partial_value = list(projections)
    sibling = [projections[0], projections[1], projections[2]]
    for bit_number in range(total_bits):
        received = partner(
            (as_sent(partial_value[0]), as_sent(partial_value[1]), as_sent(partial_value[2])),
            ("rows", "cols"),
            bit_number,
        )
        for rung_index in range(3):
            target_bit = total_bits - 1 - rung_index
            if bit_number < target_bit:
                partial_value[rung_index] = partial_value[rung_index] + received[rung_index]
            elif bit_number == target_bit:
                sibling[rung_index] = received[rung_index]
    return [entry.astype(jnp.bfloat16) for entry in sibling]


def local(probes, basis_one, basis_two, basis_three, coeff_one, coeff_two, coeff_three, leaves):
    rank_count = lax.axis_size("rank")
    rank_place = lax.axis_index("rank")
    rows_here = probes.shape[0]
    half_rows = rows_here // rank_count
    uppers = (basis_one, basis_two, basis_three)
    lowers = (coeff_one, coeff_two, coeff_three)
    current = probes
    applies = 2 * PASSES
    halfway = None
    for step_number in range(applies):
        flipped = step_number % 2 == 0
        outside = lowers if flipped else uppers
        inside = uppers if flipped else lowers
        projections = [
            jnp.einsum("nk,nc->kc", factor, current, preferred_element_type=jnp.float32)
            for factor in inside
        ]
        siblings = combine_levels(projections)
        own_rows = lax.dynamic_slice_in_dim(current, rank_place * half_rows, half_rows, 0).reshape(
            -1, LEAF, C
        )
        pattern = "bji,bjc->bic" if flipped else "bij,bjc->bic"
        leaf_term = jnp.einsum(
            pattern, leaves, own_rows, preferred_element_type=jnp.float32
        ).reshape(half_rows, C)

        def term_rows(start, count, outside=outside, siblings=siblings):
            result = jnp.dot(outside[0], siblings[0], preferred_element_type=jnp.float32)
            result = result + jnp.dot(outside[1], siblings[1], preferred_element_type=jnp.float32)
            result = result + jnp.dot(outside[2], siblings[2], preferred_element_type=jnp.float32)
            return result

        summed = lax.psum_scatter(
            term_rows(jnp.int32(0), half_rows * lax.axis_size("rank")).astype(jnp.bfloat16),
            "rank",
            scatter_dimension=0,
            tiled=True,
        ).astype(jnp.float32)
        halfway = (summed + leaf_term).astype(jnp.bfloat16)
        if step_number + 1 < applies:
            current = lax.all_gather(halfway, "rank", axis=0, tiled=True)
    return halfway


def solution(mesh):
    in_specs = (
        P(("parts", "rows", "cols"), None),
        P(("parts", "rows", "cols"), "rank"),
        P(("parts", "rows", "cols"), "rank"),
        P(("parts", "rows", "cols"), "rank"),
        P(("parts", "rows", "cols"), "rank"),
        P(("parts", "rows", "cols"), "rank"),
        P(("parts", "rows", "cols"), "rank"),
        P(("parts", "rows", "cols", "rank"), None, None),
    )
    out_specs = P(("parts", "rows", "cols", "rank"), None)
    return jax.shard_map(local, mesh=mesh, in_specs=in_specs, out_specs=out_specs, check_vma=False)
```

profile of v0, /device:TPU:0, one launch (start us, length us, event | category | flops | bytes accessed | tf_op | source)
XLA Modules:
  0.0 132.8 jit_solution(5686425325117326454)
XLA Ops:
  6.5 1.7 %convolution_convert_fusion.3 = bf16[128,128]{1,0:T(8,128)(2,1)S(1)} fusion(bf16[2048,128]{1,0:T(8,128)(2,1)} %param.11, bf16[2048,128]{1,0:T(8,128)(2,1)} %param.8), kind=kOutput, calls=%fused_computation.29 | convolution fusion | flops 67125248 | bytes 1081344 | tf_op jit(solution)/shard_map/nk,nc->kc/dot_general | solution.py:55
  8.2 3.0 %collective-permute-start.5 = (bf16[128,128]{1,0:T(8,128)(2,1)S(1)}, bf16[128,128]{1,0:T(8,128)(2,1)S(1)}, u32[]{:S(2)}, u32[]{:S(2)}) collective-permute-start(bf16[128,128]{1,0:T(8,128)(2,1)S(1)} %convolution_convert_fusion.3), channel_id=1, source_target_pairs={{0,2},{2,0},{4,6},{6,4},{8,10},{10,8},{12,14},{14,12},{1,3},{3,1},... | collective-permute-start | bytes 98312 | tf_op jit(solution)/shard_map/ppermute | solution.py:18
  11.3 0.3 fusion.20
  11.7 0.3 fusion.19
  12.0 2.1 %collective-permute-start.3 = (bf16[128,128]{1,0:T(8,128)(2,1)S(1)}, bf16[128,128]{1,0:T(8,128)(2,1)S(1)}, u32[]{:S(2)}, u32[]{:S(2)}) collective-permute-start(bf16[128,128]{1,0:T(8,128)(2,1)S(1)} %get-tuple-element.5), channel_id=1, source_target_pairs={{0,2},{2,0},{4,6},{6,4},{8,10},{10,8},{12,14},{14,12},{1,3},{3,1},... | collective-permute-start | bytes 98312 | tf_op jit(solution)/shard_map/ppermute | solution.py:18
  14.1 1.5 %collective-permute-done = bf16[128,128]{1,0:T(8,128)(2,1)S(1)} collective-permute-done((bf16[128,128]{1,0:T(8,128)(2,1)S(1)}, bf16[128,128]{1,0:T(8,128)(2,1)S(1)}, u32[]{:S(2)}, u32[]{:S(2)}) %collective-permute-start) | collective-permute-done | bytes 32800 | tf_op jit(solution)/shard_map/ppermute | solution.py:18
  15.6 1.6 %collective-permute-start.1 = (bf16[128,128]{1,0:T(8,128)(2,1)S(1)}, bf16[128,128]{1,0:T(8,128)(2,1)S(1)}, u32[]{:S(2)}, u32[]{:S(2)}) collective-permute-start(bf16[128,128]{1,0:T(8,128)(2,1)S(1)} %fusion.15), channel_id=1, source_target_pairs={{0,4},{2,6},{4,0},{6,2},{8,12},{10,14},{12,8},{14,10},{1,5},{3,7},... | collective-permute-start | bytes 98312 | tf_op jit(solution)/shard_map/ppermute | solution.py:18
  17.3 0.9 collective-permute-start.4
  18.2 0.3 fusion.28
  18.5 1.1 collective-permute-done.1
  19.6 2.8 %collective-permute-start.2 = (bf16[128,128]{1,0:T(8,128)(2,1)S(1)}, bf16[128,128]{1,0:T(8,128)(2,1)S(1)}, u32[]{:S(2)}, u32[]{:S(2)}) collective-permute-start(bf16[128,128]{1,0:T(8,128)(2,1)S(1)} %add_convert_fusion.11), channel_id=1, source_target_pairs={{0,8},{2,10},{4,12},{6,14},{8,0},{10,2},{12,4},{14,6},{1,9},{3,11}... | collective-permute-start | bytes 98312 | tf_op jit(solution)/shard_map/ppermute | solution.py:18
  22.4 0.3 fusion.27
  22.8 1.7 %collective-permute-done.2 = bf16[128,128]{1,0:T(8,128)(2,1)S(1)} collective-permute-done((bf16[128,128]{1,0:T(8,128)(2,1)S(1)}, bf16[128,128]{1,0:T(8,128)(2,1)S(1)}, u32[]{:S(2)}, u32[]{:S(2)}) %collective-permute-start.2) | collective-permute-done | bytes 32800 | tf_op jit(solution)/shard_map/ppermute | solution.py:18
  24.5 1.1 fusion.11
  25.7 0.9 copy-done.9
  27.0 7.5 %reduce-scatter.5.cloned.1.call-done = bf16[1024,128]{0,1:T(8,128)(2,1)} async-done(((bf16[2048,128]{0,1:T(8,128)(2,1)}), bf16[1024,128]{0,1:T(8,128)(2,1)}) %reduce-scatter.5.cloned.1.call-update) | async-done | bytes 262160 | tf_op jit(solution)/shard_map/reduce_scatter | solution.py:73
  34.5 1.0 add_convert_fusion.3
  35.5 2.2 %all_gather.9 = bf16[2048,128]{0,1:T(8,128)(2,1)S(1)} all-gather(bf16[1024,128]{0,1:T(8,128)(2,1)S(1)} %add_convert_fusion.3), channel_id=1, replica_groups=mesh['parts'=2,'rows'=4,'cols'=2,'rank'=2] {'rank'}, dimensions={0}, use_global_device_ids=true | all-gather | bytes 786432 | tf_op jit(solution)/shard_map/all_gather | solution.py:81
  38.3 1.8 %collective-permute-start.9 = (bf16[128,128]{0,1:T(8,128)(2,1)S(1)}, bf16[128,128]{0,1:T(8,128)(2,1)S(1)}, u32[]{:S(2)}, u32[]{:S(2)}) collective-permute-start(bf16[128,128]{0,1:T(8,128)(2,1)S(1)} %get-tuple-element.9), channel_id=1, source_target_pairs={{0,2},{2,0},{4,6},{6,4},{8,10},{10,8},{12,14},{14,12},{1,3},{3,1},... | collective-permute-start | bytes 98312 | tf_op jit(solution)/shard_map/ppermute | solution.py:18
  40.4 0.4 collective-permute-start.11
  40.8 1.7 %collective-permute-start.6 = (bf16[128,128]{0,1:T(8,128)(2,1)S(1)}, bf16[128,128]{0,1:T(8,128)(2,1)S(1)}, u32[]{:S(2)}, u32[]{:S(2)}) collective-permute-start(bf16[128,128]{0,1:T(8,128)(2,1)S(1)} %get-tuple-element.11), channel_id=1, source_target_pairs={{0,2},{2,0},{4,6},{6,4},{8,10},{10,8},{12,14},{14,12},{1,3},{3,1},... | collective-permute-start | bytes 98312 | tf_op jit(solution)/shard_map/ppermute | solution.py:18
  42.5 1.6 %collective-permute-start.10 = (bf16[128,128]{0,1:T(8,128)(2,1)S(1)}, bf16[128,128]{0,1:T(8,128)(2,1)S(1)}, u32[]{:S(2)}, u32[]{:S(2)}) collective-permute-start(bf16[128,128]{0,1:T(8,128)(2,1)S(1)} %add_convert_fusion.8), channel_id=1, source_target_pairs={{0,4},{2,6},{4,0},{6,2},{8,12},{10,14},{12,8},{14,10},{1,5},{3,7},... | collective-permute-start | bytes 98312 | tf_op jit(solution)/shard_map/ppermute | solution.py:18
  44.1 0.6 collective-permute-done.6
  44.7 1.7 %collective-permute-start.7 = (bf16[128,128]{0,1:T(8,128)(2,1)S(1)}, bf16[128,128]{0,1:T(8,128)(2,1)S(1)}, u32[]{:S(2)}, u32[]{:S(2)}) collective-permute-start(bf16[128,128]{0,1:T(8,128)(2,1)S(1)} %fusion.16), channel_id=1, source_target_pairs={{0,4},{2,6},{4,0},{6,2},{8,12},{10,14},{12,8},{14,10},{1,5},{3,7},... | collective-permute-start | bytes 98312 | tf_op jit(solution)/shard_map/ppermute | solution.py:18
  46.8 1.9 %collective-permute-done.7 = bf16[128,128]{0,1:T(8,128)(2,1)S(1)} collective-permute-done((bf16[128,128]{0,1:T(8,128)(2,1)S(1)}, bf16[128,128]{0,1:T(8,128)(2,1)S(1)}, u32[]{:S(2)}, u32[]{:S(2)}) %collective-permute-start.7) | collective-permute-done | bytes 32800 | tf_op jit(solution)/shard_map/ppermute | solution.py:18
  48.7 2.7 %collective-permute-start.8 = (bf16[128,128]{0,1:T(8,128)(2,1)S(1)}, bf16[128,128]{0,1:T(8,128)(2,1)S(1)}, u32[]{:S(2)}, u32[]{:S(2)}) collective-permute-start(bf16[128,128]{0,1:T(8,128)(2,1)S(1)} %add_convert_fusion.9), channel_id=1, source_target_pairs={{0,8},{2,10},{4,12},{6,14},{8,0},{10,2},{12,4},{14,6},{1,9},{3,11}... | collective-permute-start | bytes 98312 | tf_op jit(solution)/shard_map/ppermute | solution.py:18
  51.7 1.9 %collective-permute-done.8 = bf16[128,128]{0,1:T(8,128)(2,1)S(1)} collective-permute-done((bf16[128,128]{0,1:T(8,128)(2,1)S(1)}, bf16[128,128]{0,1:T(8,128)(2,1)S(1)}, u32[]{:S(2)}, u32[]{:S(2)}) %collective-permute-start.8) | collective-permute-done | bytes 32800 | tf_op jit(solution)/shard_map/ppermute | solution.py:18
  53.6 1.1 fusion.10
  54.8 0.7 constant_dynamic-slice_fusion.2
  55.5 1.2 copy.16
  56.7 0.3 convolution_bitcast_fusion.2
  57.1 7.2 %reduce-scatter.7.cloned.1.call-done = bf16[1024,128]{0,1:T(8,128)(2,1)} async-done(((bf16[2048,128]{0,1:T(8,128)(2,1)}), bf16[1024,128]{0,1:T(8,128)(2,1)}) %reduce-scatter.7.cloned.1.call-update) | async-done | bytes 262160 | tf_op jit(solution)/shard_map/reduce_scatter | solution.py:73
  64.2 1.0 add_convert_fusion.2
  65.2 2.2 %all_gather.10 = bf16[2048,128]{0,1:T(8,128)(2,1)S(1)} all-gather(bf16[1024,128]{0,1:T(8,128)(2,1)S(1)} %add_convert_fusion.2), channel_id=1, replica_groups=mesh['parts'=2,'rows'=4,'cols'=2,'rank'=2] {'rank'}, dimensions={0}, use_global_device_ids=true | all-gather | bytes 786432 | tf_op jit(solution)/shard_map/all_gather | solution.py:81
  67.7 0.7 copy-done.7
  68.8 1.7 %collective-permute-start.15 = (bf16[128,128]{0,1:T(8,128)(2,1)S(1)}, bf16[128,128]{0,1:T(8,128)(2,1)S(1)}, u32[]{:S(2)}, u32[]{:S(2)}) collective-permute-start(bf16[128,128]{0,1:T(8,128)(2,1)S(1)} %get-tuple-element.13), channel_id=1, source_target_pairs={{0,2},{2,0},{4,6},{6,4},{8,10},{10,8},{12,14},{14,12},{1,3},{3,1},... | collective-permute-start | bytes 98312 | tf_op jit(solution)/shard_map/ppermute | solution.py:18
  70.8 0.4 collective-permute-start.17
  71.2 1.7 %collective-permute-start.12 = (bf16[128,128]{0,1:T(8,128)(2,1)S(1)}, bf16[128,128]{0,1:T(8,128)(2,1)S(1)}, u32[]{:S(2)}, u32[]{:S(2)}) collective-permute-start(bf16[128,128]{0,1:T(8,128)(2,1)S(1)} %get-tuple-element.15), channel_id=1, source_target_pairs={{0,2},{2,0},{4,6},{6,4},{8,10},{10,8},{12,14},{14,12},{1,3},{3,1},... | collective-permute-start | bytes 98312 | tf_op jit(solution)/shard_map/ppermute | solution.py:18
  72.9 1.6 %collective-permute-start.16 = (bf16[128,128]{0,1:T(8,128)(2,1)S(1)}, bf16[128,128]{0,1:T(8,128)(2,1)S(1)}, u32[]{:S(2)}, u32[]{:S(2)}) collective-permute-start(bf16[128,128]{0,1:T(8,128)(2,1)S(1)} %add_convert_fusion.6), channel_id=1, source_target_pairs={{0,4},{2,6},{4,0},{6,2},{8,12},{10,14},{12,8},{14,10},{1,5},{3,7},... | collective-permute-start | bytes 98312 | tf_op jit(solution)/shard_map/ppermute | solution.py:18
  74.5 0.6 collective-permute-done.12
  75.1 1.8 %collective-permute-start.13 = (bf16[128,128]{0,1:T(8,128)(2,1)S(1)}, bf16[128,128]{0,1:T(8,128)(2,1)S(1)}, u32[]{:S(2)}, u32[]{:S(2)}) collective-permute-start(bf16[128,128]{0,1:T(8,128)(2,1)S(1)} %fusion.17), channel_id=1, source_target_pairs={{0,4},{2,6},{4,0},{6,2},{8,12},{10,14},{12,8},{14,10},{1,5},{3,7},... | collective-permute-start | bytes 98312 | tf_op jit(solution)/shard_map/ppermute | solution.py:18
  77.2 1.9 %collective-permute-done.13 = bf16[128,128]{0,1:T(8,128)(2,1)S(1)} collective-permute-done((bf16[128,128]{0,1:T(8,128)(2,1)S(1)}, bf16[128,128]{0,1:T(8,128)(2,1)S(1)}, u32[]{:S(2)}, u32[]{:S(2)}) %collective-permute-start.13) | collective-permute-done | bytes 32800 | tf_op jit(solution)/shard_map/ppermute | solution.py:18
  79.1 2.7 %collective-permute-start.14 = (bf16[128,128]{0,1:T(8,128)(2,1)S(1)}, bf16[128,128]{0,1:T(8,128)(2,1)S(1)}, u32[]{:S(2)}, u32[]{:S(2)}) collective-permute-start(bf16[128,128]{0,1:T(8,128)(2,1)S(1)} %add_convert_fusion.7), channel_id=1, source_target_pairs={{0,8},{2,10},{4,12},{6,14},{8,0},{10,2},{12,4},{14,6},{1,9},{3,11}... | collective-permute-start | bytes 98312 | tf_op jit(solution)/shard_map/ppermute | solution.py:18
  82.1 1.9 %collective-permute-done.14 = bf16[128,128]{0,1:T(8,128)(2,1)S(1)} collective-permute-done((bf16[128,128]{0,1:T(8,128)(2,1)S(1)}, bf16[128,128]{0,1:T(8,128)(2,1)S(1)}, u32[]{:S(2)}, u32[]{:S(2)}) %collective-permute-start.14) | collective-permute-done | bytes 32800 | tf_op jit(solution)/shard_map/ppermute | solution.py:18
  84.0 1.1 fusion.9
  85.2 0.7 constant_dynamic-slice_fusion.1
  85.9 1.2 copy.19
  87.5 7.2 %reduce-scatter.9.cloned.1.call-done = bf16[1024,128]{0,1:T(8,128)(2,1)} async-done(((bf16[2048,128]{0,1:T(8,128)(2,1)}), bf16[1024,128]{0,1:T(8,128)(2,1)}) %reduce-scatter.9.cloned.1.call-update) | async-done | bytes 262160 | tf_op jit(solution)/shard_map/reduce_scatter | solution.py:73
  94.7 1.0 add_convert_fusion.1
  95.7 2.2 %all_gather.11 = bf16[2048,128]{0,1:T(8,128)(2,1)S(1)} all-gather(bf16[1024,128]{0,1:T(8,128)(2,1)S(1)} %add_convert_fusion.1), channel_id=1, replica_groups=mesh['parts'=2,'rows'=4,'cols'=2,'rank'=2] {'rank'}, dimensions={0}, use_global_device_ids=true | all-gather | bytes 786432 | tf_op jit(solution)/shard_map/all_gather | solution.py:81
  98.5 1.7 %collective-permute-start.21 = (bf16[128,128]{0,1:T(8,128)(2,1)S(1)}, bf16[128,128]{0,1:T(8,128)(2,1)S(1)}, u32[]{:S(2)}, u32[]{:S(2)}) collective-permute-start(bf16[128,128]{0,1:T(8,128)(2,1)S(1)} %get-tuple-element.17), channel_id=1, source_target_pairs={{0,2},{2,0},{4,6},{6,4},{8,10},{10,8},{12,14},{14,12},{1,3},{3,1},... | collective-permute-start | bytes 98312 | tf_op jit(solution)/shard_map/ppermute | solution.py:18
  100.5 0.4 collective-permute-start.23
  100.9 1.7 %collective-permute-start.18 = (bf16[128,128]{0,1:T(8,128)(2,1)S(1)}, bf16[128,128]{0,1:T(8,128)(2,1)S(1)}, u32[]{:S(2)}, u32[]{:S(2)}) collective-permute-start(bf16[128,128]{0,1:T(8,128)(2,1)S(1)} %get-tuple-element.19), channel_id=1, source_target_pairs={{0,2},{2,0},{4,6},{6,4},{8,10},{10,8},{12,14},{14,12},{1,3},{3,1},... | collective-permute-start | bytes 98312 | tf_op jit(solution)/shard_map/ppermute | solution.py:18
  102.6 1.6 %collective-permute-start.22 = (bf16[128,128]{0,1:T(8,128)(2,1)S(1)}, bf16[128,128]{0,1:T(8,128)(2,1)S(1)}, u32[]{:S(2)}, u32[]{:S(2)}) collective-permute-start(bf16[128,128]{0,1:T(8,128)(2,1)S(1)} %add_convert_fusion.4), channel_id=1, source_target_pairs={{0,4},{2,6},{4,0},{6,2},{8,12},{10,14},{12,8},{14,10},{1,5},{3,7},... | collective-permute-start | bytes 98312 | tf_op jit(solution)/shard_map/ppermute | solution.py:18
  104.2 0.6 collective-permute-done.18
  104.8 1.7 %collective-permute-start.19 = (bf16[128,128]{0,1:T(8,128)(2,1)S(1)}, bf16[128,128]{0,1:T(8,128)(2,1)S(1)}, u32[]{:S(2)}, u32[]{:S(2)}) collective-permute-start(bf16[128,128]{0,1:T(8,128)(2,1)S(1)} %fusion.18), channel_id=1, source_target_pairs={{0,4},{2,6},{4,0},{6,2},{8,12},{10,14},{12,8},{14,10},{1,5},{3,7},... | collective-permute-start | bytes 98312 | tf_op jit(solution)/shard_map/ppermute | solution.py:18
  106.9 1.9 %collective-permute-done.19 = bf16[128,128]{0,1:T(8,128)(2,1)S(1)} collective-permute-done((bf16[128,128]{0,1:T(8,128)(2,1)S(1)}, bf16[128,128]{0,1:T(8,128)(2,1)S(1)}, u32[]{:S(2)}, u32[]{:S(2)}) %collective-permute-start.19) | collective-permute-done | bytes 32800 | tf_op jit(solution)/shard_map/ppermute | solution.py:18
  108.9 2.7 %collective-permute-start.20 = (bf16[128,128]{0,1:T(8,128)(2,1)S(1)}, bf16[128,128]{0,1:T(8,128)(2,1)S(1)}, u32[]{:S(2)}, u32[]{:S(2)}) collective-permute-start(bf16[128,128]{0,1:T(8,128)(2,1)S(1)} %add_convert_fusion.5), channel_id=1, source_target_pairs={{0,8},{2,10},{4,12},{6,14},{8,0},{10,2},{12,4},{14,6},{1,9},{3,11}... | collective-permute-start | bytes 98312 | tf_op jit(solution)/shard_map/ppermute | solution.py:18
  111.8 1.9 %collective-permute-done.20 = bf16[128,128]{0,1:T(8,128)(2,1)S(1)} collective-permute-done((bf16[128,128]{0,1:T(8,128)(2,1)S(1)}, bf16[128,128]{0,1:T(8,128)(2,1)S(1)}, u32[]{:S(2)}, u32[]{:S(2)}) %collective-permute-start.20) | collective-permute-done | bytes 32800 | tf_op jit(solution)/shard_map/ppermute | solution.py:18
  113.7 1.1 fusion.8
  115.1 0.8 copy-done.12
  116.3 8.1 %reduce-scatter.11.cloned.1.call-done = bf16[1024,128]{0,1:T(8,128)(2,1)} async-done(((bf16[2048,128]{0,1:T(8,128)(2,1)}), bf16[1024,128]{0,1:T(8,128)(2,1)}) %reduce-scatter.11.cloned.1.call-update) | async-done | bytes 262160 | tf_op jit(solution)/shard_map/reduce_scatter | solution.py:73
  124.4 1.0 add_convert_fusion
  125.4 0.8 copy.25
  (83 shorter events, 6.1 us)
Async XLA Ops:
  6.5 15.9 %copy-start = (bf16[2048,128]{1,0:T(8,128)(2,1)S(1)}, bf16[2048,128]{1,0:T(8,128)(2,1)}, u32[]{:S(2)}) copy-start(bf16[2048,128]{1,0:T(8,128)(2,1)} %param.13) | copy-start | bytes 1572868
  6.5 4.7 %copy-start.13 = (bf16[2048,128]{1,0:T(8,128)(2,1)S(1)}, bf16[2048,128]{1,0:T(8,128)(2,1)}, u32[]{:S(2)}) copy-start(bf16[2048,128]{1,0:T(8,128)(2,1)} %param.8) | copy-start | bytes 1572868
  6.5 4.7 %copy-start.5 = (bf16[2048,128]{1,0:T(8,128)(2,1)S(1)}, bf16[2048,128]{1,0:T(8,128)(2,1)}, u32[]{:S(2)}) copy-start(bf16[2048,128]{1,0:T(8,128)(2,1)} %param.9) | copy-start | bytes 1572868
  6.5 28.0 %reduce-scatter.5.cloned.1.call-start = ((), (), s32[]{:S(2)}) async-start(), calls=%async_computation.4 | async-start | bytes 786432 | tf_op jit(solution)/shard_map/reduce_scatter | solution.py:73
  8.2 3.5 %copy-start.4 = (bf16[2048,128]{1,0:T(8,128)(2,1)S(1)}, bf16[2048,128]{1,0:T(8,128)(2,1)}, u32[]{:S(2)}) copy-start(bf16[2048,128]{1,0:T(8,128)(2,1)} %param.10) | copy-start | bytes 1572868
  8.2 10.0 %collective-permute-start.5 = (bf16[128,128]{1,0:T(8,128)(2,1)S(1)}, bf16[128,128]{1,0:T(8,128)(2,1)S(1)}, u32[]{:S(2)}, u32[]{:S(2)}) collective-permute-start(bf16[128,128]{1,0:T(8,128)(2,1)S(1)} %convolution_convert_fusion.3), channel_id=1, source_target_pairs={{0,2},{2,0},{4,6},{6,4},{8,10},{10,8},{12,14},{14,12},{1,3},{3,1},... | collective-permute-start | bytes 98312 | tf_op jit(solution)/shard_map/ppermute | solution.py:18
  11.6 6.6 %copy-start.2 = (bf16[2048,128]{1,0:T(8,128)(2,1)S(1)}, bf16[2048,128]{1,0:T(8,128)(2,1)}, u32[]{:S(2)}) copy-start(bf16[2048,128]{1,0:T(8,128)(2,1)} %param.14) | copy-start | bytes 1572868
  11.6 4.0 %collective-permute-start = (bf16[128,128]{1,0:T(8,128)(2,1)S(1)}, bf16[128,128]{1,0:T(8,128)(2,1)S(1)}, u32[]{:S(2)}, u32[]{:S(2)}) collective-permute-start(bf16[128,128]{1,0:T(8,128)(2,1)S(1)} %get-tuple-element.7), channel_id=1, source_target_pairs={{0,2},{2,0},{4,6},{6,4},{8,10},{10,8},{12,14},{14,12},{1,3},{3,1},... | collective-permute-start | bytes 98312 | tf_op jit(solution)/shard_map/ppermute | solution.py:18
  12.0 5.2 %collective-permute-start.3 = (bf16[128,128]{1,0:T(8,128)(2,1)S(1)}, bf16[128,128]{1,0:T(8,128)(2,1)S(1)}, u32[]{:S(2)}, u32[]{:S(2)}) collective-permute-start(bf16[128,128]{1,0:T(8,128)(2,1)S(1)} %get-tuple-element.5), channel_id=1, source_target_pairs={{0,2},{2,0},{4,6},{6,4},{8,10},{10,8},{12,14},{14,12},{1,3},{3,1},... | collective-permute-start | bytes 98312 | tf_op jit(solution)/shard_map/ppermute | solution.py:18
  15.6 4.0 %collective-permute-start.1 = (bf16[128,128]{1,0:T(8,128)(2,1)S(1)}, bf16[128,128]{1,0:T(8,128)(2,1)S(1)}, u32[]{:S(2)}, u32[]{:S(2)}) collective-permute-start(bf16[128,128]{1,0:T(8,128)(2,1)S(1)} %fusion.15), channel_id=1, source_target_pairs={{0,4},{2,6},{4,0},{6,2},{8,12},{10,14},{12,8},{14,10},{1,5},{3,7},... | collective-permute-start | bytes 98312 | tf_op jit(solution)/shard_map/ppermute | solution.py:18
  17.3 5.2 %collective-permute-start.4 = (bf16[128,128]{1,0:T(8,128)(2,1)S(1)}, bf16[128,128]{1,0:T(8,128)(2,1)S(1)}, u32[]{:S(2)}, u32[]{:S(2)}) collective-permute-start(bf16[128,128]{1,0:T(8,128)(2,1)S(1)} %add_convert_fusion.10), channel_id=1, source_target_pairs={{0,4},{2,6},{4,0},{6,2},{8,12},{10,14},{12,8},{14,10},{1,5},{3,7},... | collective-permute-start | bytes 98312 | tf_op jit(solution)/shard_map/ppermute | solution.py:18
  19.6 4.9 %copy-start.1 = (bf16[2048,128]{1,0:T(8,128)(2,1)S(1)}, bf16[2048,128]{1,0:T(8,128)(2,1)}, u32[]{:S(2)}) copy-start(bf16[2048,128]{1,0:T(8,128)(2,1)} %param.12) | copy-start | bytes 1572868
  19.6 4.9 %collective-permute-start.2 = (bf16[128,128]{1,0:T(8,128)(2,1)S(1)}, bf16[128,128]{1,0:T(8,128)(2,1)S(1)}, u32[]{:S(2)}, u32[]{:S(2)}) collective-permute-start(bf16[128,128]{1,0:T(8,128)(2,1)S(1)} %add_convert_fusion.11), channel_id=1, source_target_pairs={{0,8},{2,10},{4,12},{6,14},{8,0},{10,2},{12,4},{14,6},{1,9},{3,11}... | collective-permute-start | bytes 98312 | tf_op jit(solution)/shard_map/ppermute | solution.py:18
  25.6 1.0 copy-start.9
  25.7 38.6 %reduce-scatter.7.cloned.1.call-start = ((), (), s32[]{:S(2)}) async-start(), calls=%async_computation.5 | async-start | bytes 786432 | tf_op jit(solution)/shard_map/reduce_scatter | solution.py:73
  38.3 8.1 %copy-start.3 = (bf16[2048,128]{1,0:T(8,128)(2,1)S(1)}, bf16[2048,128]{1,0:T(8,128)(2,1)}, u32[]{:S(2)}) copy-start(bf16[2048,128]{1,0:T(8,128)(2,1)} %param.11) | copy-start | bytes 1572868
  38.3 4.1 %collective-permute-start.9 = (bf16[128,128]{0,1:T(8,128)(2,1)S(1)}, bf16[128,128]{0,1:T(8,128)(2,1)S(1)}, u32[]{:S(2)}, u32[]{:S(2)}) collective-permute-start(bf16[128,128]{0,1:T(8,128)(2,1)S(1)} %get-tuple-element.9), channel_id=1, source_target_pairs={{0,2},{2,0},{4,6},{6,4},{8,10},{10,8},{12,14},{14,12},{1,3},{3,1},... | collective-permute-start | bytes 98312 | tf_op jit(solution)/shard_map/ppermute | solution.py:18
  40.4 6.1 %collective-permute-start.11 = (bf16[128,128]{0,1:T(8,128)(2,1)S(1)}, bf16[128,128]{0,1:T(8,128)(2,1)S(1)}, u32[]{:S(2)}, u32[]{:S(2)}) collective-permute-start(bf16[128,128]{0,1:T(8,128)(2,1)S(1)} %fusion.12), channel_id=1, source_target_pairs={{0,2},{2,0},{4,6},{6,4},{8,10},{10,8},{12,14},{14,12},{1,3},{3,1},... | collective-permute-start | bytes 98312 | tf_op jit(solution)/shard_map/ppermute | solution.py:18
  40.8 3.9 %collective-permute-start.6 = (bf16[128,128]{0,1:T(8,128)(2,1)S(1)}, bf16[128,128]{0,1:T(8,128)(2,1)S(1)}, u32[]{:S(2)}, u32[]{:S(2)}) collective-permute-start(bf16[128,128]{0,1:T(8,128)(2,1)S(1)} %get-tuple-element.11), channel_id=1, source_target_pairs={{0,2},{2,0},{4,6},{6,4},{8,10},{10,8},{12,14},{14,12},{1,3},{3,1},... | collective-permute-start | bytes 98312 | tf_op jit(solution)/shard_map/ppermute | solution.py:18
  42.5 8.9 %collective-permute-start.10 = (bf16[128,128]{0,1:T(8,128)(2,1)S(1)}, bf16[128,128]{0,1:T(8,128)(2,1)S(1)}, u32[]{:S(2)}, u32[]{:S(2)}) collective-permute-start(bf16[128,128]{0,1:T(8,128)(2,1)S(1)} %add_convert_fusion.8), channel_id=1, source_target_pairs={{0,4},{2,6},{4,0},{6,2},{8,12},{10,14},{12,8},{14,10},{1,5},{3,7},... | collective-permute-start | bytes 98312 | tf_op jit(solution)/shard_map/ppermute | solution.py:18
  44.7 4.0 %collective-permute-start.7 = (bf16[128,128]{0,1:T(8,128)(2,1)S(1)}, bf16[128,128]{0,1:T(8,128)(2,1)S(1)}, u32[]{:S(2)}, u32[]{:S(2)}) collective-permute-start(bf16[128,128]{0,1:T(8,128)(2,1)S(1)} %fusion.16), channel_id=1, source_target_pairs={{0,4},{2,6},{4,0},{6,2},{8,12},{10,14},{12,8},{14,10},{1,5},{3,7},... | collective-permute-start | bytes 98312 | tf_op jit(solution)/shard_map/ppermute | solution.py:18
  48.7 4.9 %copy-start.6 = (bf16[2048,128]{1,0:T(8,128)(2,1)S(1)}, bf16[2048,128]{1,0:T(8,128)(2,1)}, u32[]{:S(2)}) copy-start(bf16[2048,128]{1,0:T(8,128)(2,1)} %param.9) | copy-start | bytes 1572868
  48.7 4.9 %collective-permute-start.8 = (bf16[128,128]{0,1:T(8,128)(2,1)S(1)}, bf16[128,128]{0,1:T(8,128)(2,1)S(1)}, u32[]{:S(2)}, u32[]{:S(2)}) collective-permute-start(bf16[128,128]{0,1:T(8,128)(2,1)S(1)} %add_convert_fusion.9), channel_id=1, source_target_pairs={{0,8},{2,10},{4,12},{6,14},{8,0},{10,2},{12,4},{14,6},{1,9},{3,11}... | collective-permute-start | bytes 98312 | tf_op jit(solution)/shard_map/ppermute | solution.py:18
  54.7 40.0 %reduce-scatter.9.cloned.1.call-start = ((), (), s32[]{:S(2)}) async-start(), calls=%async_computation.6 | async-start | bytes 786432 | tf_op jit(solution)/shard_map/reduce_scatter | solution.py:73
  55.5 1.2 copy-start.10
  67.4 1.0 copy-start.7
  68.8 4.1 %collective-permute-start.15 = (bf16[128,128]{0,1:T(8,128)(2,1)S(1)}, bf16[128,128]{0,1:T(8,128)(2,1)S(1)}, u32[]{:S(2)}, u32[]{:S(2)}) collective-permute-start(bf16[128,128]{0,1:T(8,128)(2,1)S(1)} %get-tuple-element.13), channel_id=1, source_target_pairs={{0,2},{2,0},{4,6},{6,4},{8,10},{10,8},{12,14},{14,12},{1,3},{3,1},... | collective-permute-start | bytes 98312 | tf_op jit(solution)/shard_map/ppermute | solution.py:18
  70.8 6.1 %collective-permute-start.17 = (bf16[128,128]{0,1:T(8,128)(2,1)S(1)}, bf16[128,128]{0,1:T(8,128)(2,1)S(1)}, u32[]{:S(2)}, u32[]{:S(2)}) collective-permute-start(bf16[128,128]{0,1:T(8,128)(2,1)S(1)} %fusion.13), channel_id=1, source_target_pairs={{0,2},{2,0},{4,6},{6,4},{8,10},{10,8},{12,14},{14,12},{1,3},{3,1},... | collective-permute-start | bytes 98312 | tf_op jit(solution)/shard_map/ppermute | solution.py:18
  71.2 3.9 %collective-permute-start.12 = (bf16[128,128]{0,1:T(8,128)(2,1)S(1)}, bf16[128,128]{0,1:T(8,128)(2,1)S(1)}, u32[]{:S(2)}, u32[]{:S(2)}) collective-permute-start(bf16[128,128]{0,1:T(8,128)(2,1)S(1)} %get-tuple-element.15), channel_id=1, source_target_pairs={{0,2},{2,0},{4,6},{6,4},{8,10},{10,8},{12,14},{14,12},{1,3},{3,1},... | collective-permute-start | bytes 98312 | tf_op jit(solution)/shard_map/ppermute | solution.py:18
  72.9 8.9 %collective-permute-start.16 = (bf16[128,128]{0,1:T(8,128)(2,1)S(1)}, bf16[128,128]{0,1:T(8,128)(2,1)S(1)}, u32[]{:S(2)}, u32[]{:S(2)}) collective-permute-start(bf16[128,128]{0,1:T(8,128)(2,1)S(1)} %add_convert_fusion.6), channel_id=1, source_target_pairs={{0,4},{2,6},{4,0},{6,2},{8,12},{10,14},{12,8},{14,10},{1,5},{3,7},... | collective-permute-start | bytes 98312 | tf_op jit(solution)/shard_map/ppermute | solution.py:18
  75.1 4.0 %collective-permute-start.13 = (bf16[128,128]{0,1:T(8,128)(2,1)S(1)}, bf16[128,128]{0,1:T(8,128)(2,1)S(1)}, u32[]{:S(2)}, u32[]{:S(2)}) collective-permute-start(bf16[128,128]{0,1:T(8,128)(2,1)S(1)} %fusion.17), channel_id=1, source_target_pairs={{0,4},{2,6},{4,0},{6,2},{8,12},{10,14},{12,8},{14,10},{1,5},{3,7},... | collective-permute-start | bytes 98312 | tf_op jit(solution)/shard_map/ppermute | solution.py:18
  79.1 4.9 %collective-permute-start.14 = (bf16[128,128]{0,1:T(8,128)(2,1)S(1)}, bf16[128,128]{0,1:T(8,128)(2,1)S(1)}, u32[]{:S(2)}, u32[]{:S(2)}) collective-permute-start(bf16[128,128]{0,1:T(8,128)(2,1)S(1)} %add_convert_fusion.7), channel_id=1, source_target_pairs={{0,8},{2,10},{4,12},{6,14},{8,0},{10,2},{12,4},{14,6},{1,9},{3,11}... | collective-permute-start | bytes 98312 | tf_op jit(solution)/shard_map/ppermute | solution.py:18
  85.2 39.2 %reduce-scatter.11.cloned.1.call-start = ((), (), s32[]{:S(2)}) async-start(), calls=%async_computation.7 | async-start | bytes 786432 | tf_op jit(solution)/shard_map/reduce_scatter | solution.py:73
  85.9 1.2 copy-start.11
  98.5 4.1 %collective-permute-start.21 = (bf16[128,128]{0,1:T(8,128)(2,1)S(1)}, bf16[128,128]{0,1:T(8,128)(2,1)S(1)}, u32[]{:S(2)}, u32[]{:S(2)}) collective-permute-start(bf16[128,128]{0,1:T(8,128)(2,1)S(1)} %get-tuple-element.17), channel_id=1, source_target_pairs={{0,2},{2,0},{4,6},{6,4},{8,10},{10,8},{12,14},{14,12},{1,3},{3,1},... | collective-permute-start | bytes 98312 | tf_op jit(solution)/shard_map/ppermute | solution.py:18
  100.5 6.1 %collective-permute-start.23 = (bf16[128,128]{0,1:T(8,128)(2,1)S(1)}, bf16[128,128]{0,1:T(8,128)(2,1)S(1)}, u32[]{:S(2)}, u32[]{:S(2)}) collective-permute-start(bf16[128,128]{0,1:T(8,128)(2,1)S(1)} %fusion.14), channel_id=1, source_target_pairs={{0,2},{2,0},{4,6},{6,4},{8,10},{10,8},{12,14},{14,12},{1,3},{3,1},... | collective-permute-start | bytes 98312 | tf_op jit(solution)/shard_map/ppermute | solution.py:18
  100.9 3.9 %collective-permute-start.18 = (bf16[128,128]{0,1:T(8,128)(2,1)S(1)}, bf16[128,128]{0,1:T(8,128)(2,1)S(1)}, u32[]{:S(2)}, u32[]{:S(2)}) collective-permute-start(bf16[128,128]{0,1:T(8,128)(2,1)S(1)} %get-tuple-element.19), channel_id=1, source_target_pairs={{0,2},{2,0},{4,6},{6,4},{8,10},{10,8},{12,14},{14,12},{1,3},{3,1},... | collective-permute-start | bytes 98312 | tf_op jit(solution)/shard_map/ppermute | solution.py:18
  102.6 8.9 %collective-permute-start.22 = (bf16[128,128]{0,1:T(8,128)(2,1)S(1)}, bf16[128,128]{0,1:T(8,128)(2,1)S(1)}, u32[]{:S(2)}, u32[]{:S(2)}) collective-permute-start(bf16[128,128]{0,1:T(8,128)(2,1)S(1)} %add_convert_fusion.4), channel_id=1, source_target_pairs={{0,4},{2,6},{4,0},{6,2},{8,12},{10,14},{12,8},{14,10},{1,5},{3,7},... | collective-permute-start | bytes 98312 | tf_op jit(solution)/shard_map/ppermute | solution.py:18
  104.8 4.0 %collective-permute-start.19 = (bf16[128,128]{0,1:T(8,128)(2,1)S(1)}, bf16[128,128]{0,1:T(8,128)(2,1)S(1)}, u32[]{:S(2)}, u32[]{:S(2)}) collective-permute-start(bf16[128,128]{0,1:T(8,128)(2,1)S(1)} %fusion.18), channel_id=1, source_target_pairs={{0,4},{2,6},{4,0},{6,2},{8,12},{10,14},{12,8},{14,10},{1,5},{3,7},... | collective-permute-start | bytes 98312 | tf_op jit(solution)/shard_map/ppermute | solution.py:18
  108.8 4.9 %copy-start.8 = (bf16[2048,128]{1,0:T(8,128)(2,1)S(1)}, bf16[2048,128]{1,0:T(8,128)(2,1)}, u32[]{:S(2)}) copy-start(bf16[2048,128]{1,0:T(8,128)(2,1)} %param.9) | copy-start | bytes 1572868
  108.9 4.9 %collective-permute-start.20 = (bf16[128,128]{0,1:T(8,128)(2,1)S(1)}, bf16[128,128]{0,1:T(8,128)(2,1)S(1)}, u32[]{:S(2)}, u32[]{:S(2)}) collective-permute-start(bf16[128,128]{0,1:T(8,128)(2,1)S(1)} %add_convert_fusion.5), channel_id=1, source_target_pairs={{0,8},{2,10},{4,12},{6,14},{8,0},{10,2},{12,4},{14,6},{1,9},{3,11}... | collective-permute-start | bytes 98312 | tf_op jit(solution)/shard_map/ppermute | solution.py:18
  114.9 1.0 copy-start.12
Sparse Core Ops, SparseCore 0:
  25.8 8.6 reduce-scatter.4
  54.8 9.3 reduce-scatter.6
  85.3 9.3 reduce-scatter.8
  115.0 9.3 reduce-scatter.10
where the time goes:
time: 133 us
  waiting for transfers between devices  47.7 us (36%)
  starting transfers between devices  40.3 us (30%)
  between operations  13.5 us (10%)
  matrix products  12.9 us (10%)
  local copies, waits for them, and re-layouts  7.63 us (6%)
  blocking collectives  6.54 us (5%)
  other arithmetic  4.14 us (3%)
    ppermute x24, starting transfers between devices, partner(): return lax.ppermute(value, axis, pairs)  40.1 us
    reduce_scatter x4, waiting for transfers between devices, local(): lax.psum_scatter(term_rows(jnp.int32(0), half_rows * lax.axis_size('rank'...  30 us
    ppermute x24, waiting for transfers between devices, partner(): return lax.ppermute(value, axis, pairs)  17.7 us
    all_gather x3, blocking collectives, local(): current = lax.all_gather(halfway, 'rank', axis=0, tiled=True)  6.54 us
    dot_general x12, matrix products, local(): jnp.einsum('nk,nc->kc', factor, current, preferred_element_type=jnp.float32)  4.9 us
    dot_general x4, matrix products, term_rows(): jnp.dot(outside[0], siblings[0], preferred_element_type=jnp.float32)  4.45 us
    dynamic_slice x7, local copies, waits for them, and re-layouts, local(): lax.dynamic_slice_in_dim(current, rank_place * half_rows, half_rows, 0)  4.03 us
    convert_element_type x4, other arithmetic, local(): halfway = (summed + leaf_term).astype(jnp.bfloat16)  4 us
  transfers between devices with their start and end apart: 28, of which 16 were waited for; matrix products, arithmetic and copies ran while one was open for 7% of the time, Pallas kernels for 0%

commit v1 on v0

v1 whole, which is shorter than its diff:
```python
import functools

import jax
import jax.numpy as jnp
from jax import lax
from jax.experimental import pallas as pl
from jax.experimental.pallas import tpu as pltpu
from jax.sharding import PartitionSpec as P

PASSES = 2
LEVELS = 3
MESH = pl.DeviceIdType.MESH
F32 = jnp.float32


def flip(value, mask):
    bit = 1
    out = value
    while bit <= mask:
        if mask & bit:
            out = out + (1 - 2 * lax.rem(lax.div(value, jnp.int32(bit)), jnp.int32(2))) * bit
        bit *= 2
    return out


def make_stages(bits):
    stages = []
    for level in range(1, LEVELS + 1):
        reduce_bits = bits - level
        rounds = []
        bit = 0
        while bit < reduce_bits:
            if bit + 1 < reduce_bits:
                rounds.append([1 << bit, 2 << bit, 3 << bit])
                bit += 2
            else:
                rounds.append([1 << bit])
                bit += 1
        rounds.append([1 << reduce_bits])
        stages.append(rounds)
    return stages


def tdot(a, b):
    return lax.dot_general(a, b, (((0,), (0,)), ((), ())), preferred_element_type=F32)


def dot(a, b):
    return jnp.dot(a, b, preferred_element_type=F32)


def kernel(stages, cols_n, probes, b1, b2, b3, c1, c2, c3, leaves, out,
           fac, far, z_own, z_far, lv, acc, proj, rbuf, sbuf, lsem, fss, frs, ss, rs):
    uppers, lowers = (b1, b2, b3), (c1, c2, c3)
    half = z_own.shape[0]
    leaf = leaves.shape[1]
    part = lax.axis_index("parts")
    position = lax.axis_index("rows") * cols_n + lax.axis_index("cols")
    rank = lax.axis_index("rank")

    def peer(mask):
        other = flip(position, mask)
        return (part, lax.div(other, jnp.int32(cols_n)), lax.rem(other, jnp.int32(cols_n)), rank)

    twin = (part, lax.axis_index("rows"), lax.axis_index("cols"), 1 - rank)
    masks = sorted({m for rounds in stages for masks in rounds for m in masks})
    peers = {m: peer(m) for m in masks}

    barrier = pltpu.get_barrier_semaphore()
    for device in [twin] + list(peers.values()):
        pl.semaphore_signal(barrier, inc=1, device_id=device, device_id_type=MESH)

    own_rows = pl.ds(pl.multiple_of(rank * half, half), half)
    far_rows = pl.ds(pl.multiple_of((1 - rank) * half, half), half)
    loads = []

    def load(src, dst):
        copy = pltpu.make_async_copy(src, dst, lsem.at[len(loads)])
        copy.start()
        loads.append(copy)
        return copy

    load_z = [load(probes.at[own_rows], z_own), load(probes.at[far_rows], z_far)]
    load_up = [
        (load(uppers[i].at[own_rows], fac.at[i, 0]), load(uppers[i].at[far_rows], far.at[i]))
        for i in range(LEVELS)
    ]
    load_leaves = load(leaves, lv)
    load_low = [load(lowers[i].at[own_rows], fac.at[LEVELS + i, 0]) for i in range(LEVELS)]

    for copy in load_z:
        copy.wait()
    started = []
    counts = {"r": 0, "s": 0}

    def send(src, device):
        slot = counts["r"]
        counts["r"] += 1
        copy = pltpu.make_async_remote_copy(
            src_ref=src, dst_ref=rbuf.at[slot], send_sem=ss.at[slot], recv_sem=rs.at[slot],
            device_id=device, device_id_type=MESH)
        copy.start()
        started.append(copy)
        return copy, slot

    def stage_out(value):
        slot = counts["s"]
        counts["s"] += 1
        sbuf[slot] = value.astype(sbuf.dtype)
        return sbuf.at[slot]

    trade = [None] * (2 * LEVELS)
    applies = 2 * PASSES
    total_rounds = max(len(rounds) for rounds in stages)
    for step in range(applies):
        flipped = step % 2 == 0
        inside = 0 if flipped else LEVELS
        outside = LEVELS if flipped else 0
        twin_part = [None] * LEVELS
        if step == 0:
            for i in range(LEVELS):
                for copy in load_up[i]:
                    copy.wait()
                proj[i] = tdot(fac[i, 0], z_own[...]) + tdot(far[i], z_far[...])
            pl.semaphore_wait(barrier, 1 + len(masks))
        else:
            z = z_own[...]
            for i in range(LEVELS):
                twin_part[i] = send(stage_out(tdot(fac[inside + i, 1], z)), twin)
            for i in range(LEVELS):
                proj[i] = tdot(fac[inside + i, 0], z)

        in_flight = [None] * LEVELS
        finals = []

        def own_term(i, slot, outside=outside):
            if step == 0:
                load_low[i].wait()
            acc[...] += dot(fac[outside + i, 0], rbuf[slot])

        def twin_term(i, copy, slot, outside=outside):
            if step <= 1:
                trade[outside + i].wait_recv()
            copy.wait_recv()
            acc[...] += dot(fac[outside + i, 1], rbuf[slot])

        for turn in range(total_rounds + 1):
            order = range(LEVELS) if turn < total_rounds else reversed(range(LEVELS))
            for i in order:
                rounds = stages[i]
                if turn == 0:
                    if twin_part[i] is not None:
                        copy, slot = twin_part[i]
                        copy.wait_recv()
                        proj[i] += rbuf[slot].astype(F32)
                elif turn <= len(rounds):
                    for copy, _ in in_flight[i]:
                        copy.wait_recv()
                    if turn < len(rounds):
                        total = proj[i]
                        for _, slot in in_flight[i]:
                            total = total + rbuf[slot].astype(F32)
                        proj[i] = total
                    else:
                        _, slot = in_flight[i][0]
                        forward = send(rbuf.at[slot], twin)
                        own_term(i, slot)
                        for item in finals:
                            twin_term(*item)
                        finals = [(i,) + forward]
                if turn < len(rounds):
                    source = stage_out(proj[i])
                    in_flight[i] = [send(source, peers[m]) for m in rounds[turn]]
            if turn == 0:
                if step == 0:
                    for i in range(2 * LEVELS):
                        k = (i + LEVELS) % (2 * LEVELS)
                        src = far.at[k] if k < LEVELS else lowers[k - LEVELS].at[far_rows]
                        trade[k] = pltpu.make_async_remote_copy(
                            src_ref=src, dst_ref=fac.at[k, 1], send_sem=fss.at[k], recv_sem=frs.at[k],
                            device_id=twin, device_id_type=MESH)
                        trade[k].start()
                        started.append(trade[k])
                    load_leaves.wait()
                for q in range(half // leaf):
                    rows = slice(q * leaf, (q + 1) * leaf)
                    piece = z_own[rows]
                    acc[rows] = tdot(lv[q], piece) if flipped else dot(lv[q], piece)
        for item in finals:
            twin_term(*item)
        if step + 1 < applies:
            z_own[...] = acc[...].astype(z_own.dtype)
        else:
            out[...] = acc[...].astype(out.dtype)
    for copy in started:
        copy.wait_send()


def local(mesh, probes, *rest):
    rows_n, cols_n = mesh.shape["rows"], mesh.shape["cols"]
    stages = make_stages((rows_n * cols_n).bit_length() - 1)
    factor, leaves = rest[0], rest[-1]
    half = probes.shape[0] // mesh.shape["rank"]
    c = probes.shape[1]
    k = factor.shape[1]
    applies = 2 * PASSES
    n_recv = applies * (sum(len(m) for rounds in stages for m in rounds) + LEVELS) + (applies - 1) * LEVELS
    n_send = applies * sum(len(rounds) for rounds in stages) + (applies - 1) * LEVELS
    bf16 = probes.dtype
    return pl.pallas_call(
        functools.partial(kernel, stages, cols_n),
        out_shape=jax.ShapeDtypeStruct((half, c), bf16),
        in_specs=[pl.BlockSpec(memory_space=pl.ANY)] * (2 + 2 * LEVELS),
        out_specs=pl.BlockSpec(memory_space=pltpu.VMEM),
        scratch_shapes=[
            pltpu.VMEM((2 * LEVELS, 2, half, k), bf16),
            pltpu.VMEM((LEVELS, half, k), bf16),
            pltpu.VMEM((half, c), bf16),
            pltpu.VMEM((half, c), bf16),
            pltpu.VMEM(leaves.shape, bf16),
            pltpu.VMEM((half, c), F32),
            pltpu.VMEM((LEVELS, k, c), F32),
            pltpu.VMEM((n_recv, k, c), bf16),
            pltpu.VMEM((n_send, k, c), bf16),
            pltpu.SemaphoreType.DMA((3 + 3 * LEVELS,)),
            pltpu.SemaphoreType.DMA((2 * LEVELS,)),
            pltpu.SemaphoreType.DMA((2 * LEVELS,)),
            pltpu.SemaphoreType.DMA((n_recv,)),
            pltpu.SemaphoreType.DMA((n_recv,)),
        ],
        compiler_params=pltpu.CompilerParams(collective_id=0, has_side_effects=True),
    )(probes, *rest)


def solution(mesh):
    rows = ("parts", "rows", "cols")
    in_specs = (P(rows, None),) + (P(rows, "rank"),) * (2 * LEVELS) + (P(rows + ("rank",), None, None),)
    out_specs = P(rows + ("rank",), None)
    return jax.shard_map(
        functools.partial(local, mesh), mesh=mesh, in_specs=in_specs, out_specs=out_specs, check_vma=False)
```

time: 133 us -> 48.3 us (0.36)
  waiting for transfers between devices: 47.7 us -> 0 us
  Pallas kernels: 0 us -> 46.3 us
  starting transfers between devices: 40.3 us -> 0 us
  between operations: 13.5 us -> 0.01 us
  matrix products: 12.9 us -> 0 us
  blocking collectives: 6.54 us -> 0 us
  local copies, waits for them, and re-layouts: 7.63 us -> 1.67 us
  other arithmetic: 4.14 us -> 0 us
    pallas_call x0 -> x1, Pallas kernels: none -> 46.3 us  [local(): pl.pallas_call(functools.partial(kernel, stages, cols_n), out_shape=jax.S...]
    ppermute x24 -> x0, starting transfers between devices: 40.1 us -> none  [partner(): return lax.ppermute(value, axis, pairs)]
    reduce_scatter x4 -> x0, waiting for transfers between devices: 30 us -> none  [local(): lax.psum_scatter(term_rows(jnp.int32(0), half_rows * lax.axis_size('rank'...]
    ppermute x24 -> x0, waiting for transfers between devices: 17.7 us -> none  [partner(): return lax.ppermute(value, axis, pairs)]
    dot_general x28 -> x0, matrix products: 12.9 us -> none  [the longest x12 4.9 us: local(): jnp.einsum('nk,nc->kc', factor, current, preferred_element_type=jnp.float32)]
    all_gather x3 -> x0, blocking collectives: 6.54 us -> none  [local(): current = lax.all_gather(halfway, 'rank', axis=0, tiled=True)]
    convert_element_type x16 -> x0, other arithmetic: 4.14 us -> none  [the longest x4 4 us: local(): halfway = (summed + leaf_term).astype(jnp.bfloat16)]
    dynamic_slice x7 -> x0, local copies, waits for them, and re-layouts: 4.03 us -> none  [local(): lax.dynamic_slice_in_dim(current, rank_place * half_rows, half_rows, 0)]
  transfers between devices with their start and end apart: 28 -> 0, of which waited for: 16 -> 0; matrix products, arithmetic and copies ran while one was open for 7% -> 0% of each run, Pallas kernels for 0% -> 0%
where the time goes in v1:
time: 48.3 us; the launch traced here: 48 us
  Pallas kernels  46.3 us (96%)
  local copies, waits for them, and re-layouts  1.67 us (3%)
    pallas_call x1, Pallas kernels, local(): pl.pallas_call(functools.partial(kernel, stages, cols_n), out_shape=jax.S...  46.3 us
    unnamed x1, local copies, waits for them, and re-layouts  1.67 us

profile of v1, /device:TPU:0, one launch (start us, length us, event | category | flops | bytes accessed | tf_op | source)
XLA Modules:
  0.0 48.0 jit_solution(14689968933782807634)
XLA Ops:
  0.0 46.3 %shard_map.82 = bf16[1024,128]{1,0:T(8,128)(2,1)} custom-call(bf16[2048,128]{1,0:T(8,128)(2,1)} %probes.1, bf16[2048,128]{1,0:T(8,128)(2,1)} %b1.1, bf16[2048,128]{1,0:T(8,128)(2,1)} %b2.1, bf16[2048,128]{1,0:T(8,128)(2,1)} %b3.1, bf16[2048,128]{1,0:T(8,128)(2,1)} %c1.1, bf16[2048,128]{1,0:T(8,128)(2,1)} %c2.1, bf16[2048,128]{1,0:T(8,128)(2,1)} %c3.1, ...), custom_call_target="tpu_custom_call" | custom-call | tf_op jit(solution)/shard_map/pallas_call | solution.py:210
  46.3 1.7 %copy.10 = bf16[1024,128]{1,0:T(8,128)(2,1)} copy(bf16[1024,128]{1,0:T(8,128)(2,1)} %shard_map.82) | data formatting | bytes 524288
